TPU v7x, 256 devices: a whole 4x4x8 slice. The times are simulated.
256 devices in a mesh: region: 32 (over x, z), member: 8 (over y, core).
Axes of the slice: x: 4, y: 4, z: 8, core: 2. Of those that a mesh axis runs over, the one named last changes fastest.
Arguments:
- ensemble: bfloat16 [80, 524288], P('member', 'region'), may hold values from -6 to 6
- obs_value: float32 [8192, 128], P(('region', 'member')), may hold values from -8 to 8
- obs_var: float32 [8192, 128], P(('region', 'member')), may hold values from 0.1 to 1
- obs_point: int32 [8192, 128], P(('region', 'member')), may hold values from 0 to 16383
- owned_blocks: int32 [4096], P('region'), may hold values from 0 to 4095, each once
- infl_mean: float32 [4096], replicated, may hold values from 0.6 to 1.6
- infl_var: float32 [4096], replicated, may hold values from 0.0001 to 0.1
Outputs:
- inflated: bfloat16 [80, 524288], P('member', 'region')
- infl_post: float32 [4096], P(('region', 'member'))
Inputs may be any that keep to these rules, and one draw needn't show every extreme that they name: `obs_point`: index among the 16384 points of the observation's region; the observation belongs to the block of that point's slot. `owned_blocks`: every block id appears exactly once.
All inputs are finite; a program needn't handle non-finite values.
Results may differ from a plain program's by a relative error of at most 0.001.
Values sent between devices are 32-bit elements; how exact they have to be, the bound alone decides.
A program may use at most 64 MiB of HBM per device.

v0:
```python
import functools

import jax
import jax.numpy as jnp
from jax import lax
from jax.experimental import pallas as pl
from jax.experimental.pallas import tpu as pltpu
from jax.sharding import PartitionSpec as P

LANES = 128
MESH = pl.DeviceIdType.MESH
F32 = jnp.float32
BF16 = jnp.bfloat16
NT = (((1,), (1,)), ((), ()))


def split(value, parts):
    terms = []
    for _ in range(parts):
        term = value.astype(BF16).astype(F32)
        terms.append(term)
        value = value - term
    return terms


def scatter(value_ref, var_ref, point_ref, acc, row_acc, half, first_part):
    rows = point_ref.shape[0]
    step = 8
    low_ids = lax.broadcasted_iota(jnp.int32, (half, LANES), 0)
    col_ids = lax.broadcasted_iota(jnp.int32, (2 * LANES, LANES), 0)
    slot_ids = lax.broadcasted_iota(jnp.int32, (2 * half, LANES), 0)

    def chunk(first):
        point = point_ref[pl.ds(first, step), :]
        slot = point >> 7
        upper = (slot >= half).astype(jnp.int32)
        low = slot - half * upper
        col = (point & (LANES - 1)) + LANES * upper
        y = split(value_ref[pl.ds(first, step), :], 2)
        exact = y[0] + y[1]
        raw = var_ref[pl.ds(first, step), :]
        v = split(raw, 2)
        terms = [jnp.ones_like(raw)] + y + v
        row_terms = v + split(raw * raw, 3) + split(exact * exact, 3)
        left, right, hots = [], [], []
        row_left = []
        for r in range(step):
            here = slice(r, r + 1)
            hot = (low_ids == low[here, :]).astype(F32).astype(BF16)
            blocks = []
            for term in terms:
                wide = jnp.broadcast_to(term[here, :], (16, LANES)).astype(BF16)
                blocks.append(hot * jnp.concatenate([wide] * (half // 16), 0))
            left.append(jnp.concatenate(blocks, 0))
            right.append((col_ids == col[here, :]).astype(F32).astype(BF16))
            hots.append((slot_ids == slot[here, :]).astype(F32).astype(BF16))
            row_left.append(jnp.concatenate([term[here, :] for term in row_terms], 0))
        points = lax.dot_general(
            jnp.concatenate(left, 1), jnp.concatenate(right, 1), NT, preferred_element_type=F32
        )
        by_slot = lax.dot_general(
            jnp.concatenate(row_left, 1).astype(BF16), jnp.concatenate(hots, 1), NT,
            preferred_element_type=F32,
        )
        return points, by_slot

    def add(i):
        points, by_slot = chunk(pl.multiple_of(i * step, step))
        acc[...] += points
        row_acc[...] += by_slot

    if first_part:
        points, by_slot = chunk(0)
        acc[...] = points
        row_acc[...] = by_slot
        pl.loop(1, rows // step // 2)(add)
    else:
        pl.loop(rows // step // 2, rows // step)(add)


def kernel(
    n_region, n_member, members,
    ens_hbm, value_hbm, var_hbm, point_hbm, owned_hbm, pmean_hbm, pvar_hbm,
    out_ref, post_ref,
    ens, value, var, point, owned, pmean, pvar,
    part, rs_recv, means, factors, acc, row_acc, place, place_recv,
    in_sem, rs_send, rs_got, mean_send, mean_got, f_send, f_got, pl_send, pl_got,
):
    region = lax.axis_index("region")
    me = lax.axis_index("member")
    slots = owned.shape[1]
    own = slots // n_member
    half = slots // 2
    devices = n_region * n_member
    flat = region * n_member + me

    def device(i):
        there = lax.rem(flat + i, devices)
        return there, (there // n_member, lax.rem(there, n_member))

    def peer(i):
        return {"member": lax.rem(me + i, n_member)}

    barrier = pltpu.get_barrier_semaphore()
    for i in range(1, devices):
        pl.semaphore_signal(barrier, inc=1, device_id=device(i)[1], device_id_type=MESH)
    pairs = (
        (ens_hbm, ens), (point_hbm, point), (value_hbm, value), (var_hbm, var),
        (owned_hbm, owned), (pmean_hbm, pmean), (pvar_hbm, pvar),
    )
    loads = [pltpu.make_async_copy(s, d, in_sem.at[i]) for i, (s, d) in enumerate(pairs)]
    for load in loads:
        load.start()
    loads[0].wait()

    @pl.loop(0, n_member)
    def _(k):
        @pl.loop(0, own, unroll=8)
        def _(r):
            start = pl.multiple_of((k * own + r) * LANES, LANES)
            wide = ens[:, pl.ds(start, LANES)].astype(F32)
            part[k, pl.ds(r, 1), :] = jnp.sum(wide, 0, keepdims=True)
            part[k, pl.ds(own + r, 1), :] = jnp.sum(wide * wide, 0, keepdims=True)

    for load in loads[1:]:
        load.wait()
    scatter(value, var, point, acc, row_acc, half, True)
    pl.semaphore_wait(barrier, devices - 1)

    def reduce_copies(first, count, which):
        copies = []
        for i in range(1, n_member):
            copy = pltpu.make_async_remote_copy(
                part.at[lax.rem(me + i, n_member), pl.ds(first, count), :],
                rs_recv.at[i, pl.ds(first, count), :],
                rs_send.at[which, i], rs_got.at[which, i],
                device_id=peer(i), device_id_type=MESH,
            )
            copy.start()
            copies.append(copy)
        return copies

    rs = reduce_copies(0, 2 * own, 0)
    scatter(value, var, point, acc, row_acc, half, False)

    for index, (first, last) in enumerate(((0, 1), (1, 3), (3, 5))):
        both = acc[first * half : (first + 1) * half, :]
        for other in range(first + 1, last):
            both = both + acc[other * half : (other + 1) * half, :]
        table = jnp.concatenate([both[:, :LANES], both[:, LANES:]], 0)
        for k in range(n_member):
            part[k, (2 + index) * own : (3 + index) * own, :] = table[k * own : (k + 1) * own]
    sums = row_acc[...]
    rows = jnp.concatenate(
        [
            sums[0:1] + sums[1:2],
            sums[2:3] + sums[3:4] + sums[4:5],
            sums[5:6] + sums[6:7] + sums[7:8],
            jnp.zeros((5, slots), F32),
        ],
        0,
    )
    for k in range(n_member):
        part[k, 5 * own :, :] = rows

    rs_rest = reduce_copies(2 * own, 3 * own + 8, 1)

    block = owned[...]
    groups = pmean.shape[0]
    lane_hot = (
        lax.broadcasted_iota(jnp.int32, (LANES, slots), 0) == (block & (LANES - 1))
    ).astype(F32).astype(BF16)
    table = jnp.concatenate(split(pmean[...], 3) + split(pvar[...], 3), 0).astype(BF16)
    picked = jnp.dot(table, lane_hot, preferred_element_type=F32)
    in_group = lax.broadcasted_iota(jnp.int32, (groups, slots), 0) == (block >> 7)

    def pick(first):
        total = picked[first * groups : (first + 1) * groups]
        for i in (1, 2):
            total = total + picked[(first + i) * groups : (first + i + 1) * groups]
        return jnp.sum(jnp.where(in_group, total, 0.0), 0, keepdims=True)

    prior_mean, prior_var = pick(0), pick(3)
    share = groups * LANES // devices
    lane = lax.broadcasted_iota(jnp.int32, (1, slots), 1)
    target = lax.broadcasted_iota(jnp.int32, (devices, slots), 0) == jnp.where(
        lane // own == me, block // share, -1
    )
    spots = (
        lax.broadcasted_iota(jnp.int32, (LANES, slots), 0) == lax.rem(block, share)
    ).astype(F32).astype(BF16)
    mine = lax.broadcasted_iota(jnp.int32, (own, slots), 1) == (
        lax.broadcasted_iota(jnp.int32, (own, slots), 0) + own * me
    )

    for copy in rs:
        copy.wait_recv()

    def reduced(first, last):
        total = part[me, first:last, :]
        for i in range(1, n_member):
            total = total + rs_recv[i, first:last, :]
        return total

    both = reduced(0, 2 * own)
    mean = both[:own] / members
    means[me] = mean
    ag = []
    for i in range(1, n_member):
        copy = pltpu.make_async_remote_copy(
            means.at[me], means.at[me], mean_send.at[i], mean_got.at[i],
            device_id=peer(i), device_id_type=MESH,
        )
        copy.start()
        ag.append(copy)
    spread = (both[own:] - members * mean * mean) / (members - 1)
    for copy in rs_rest:
        copy.wait_recv()
    count = reduced(2 * own, 3 * own)
    y_sum = reduced(3 * own, 4 * own)
    v_sum = reduced(4 * own, 5 * own)
    by_slot = reduced(5 * own, 5 * own + 8)

    def to_row(table):
        column = jnp.sum(table, axis=1, keepdims=True)
        return jnp.sum(jnp.where(mine, column, 0.0), axis=0, keepdims=True)

    seen = count * spread
    so, soo = by_slot[0:1], by_slot[1:2]
    sd = by_slot[2:3] + to_row(mean * (count * mean - 2.0 * y_sum))
    sp, spp, spo = to_row(seen), to_row(seen * spread), to_row(v_sum * spread)
    weight = 2.0 * prior_mean * prior_mean * (1.0 + spp) + 4.0 * prior_mean * spo + 2.0 * soo
    post = jnp.maximum(
        (prior_mean * weight + prior_var * sp * (sd - so)) / (weight + prior_var * sp * sp), 1.0
    )

    sent = jnp.concatenate([jnp.where(target, term, 0.0) for term in split(post, 3)], 0)
    placed = lax.dot_general(sent.astype(BF16), spots, NT, preferred_element_type=F32)
    placed = placed[:devices] + placed[devices : 2 * devices] + placed[2 * devices :]
    for d in range(devices):
        place[d] = placed[d : d + 1]
    column = jnp.sum(jnp.where(mine, post, 0.0), axis=1, keepdims=True)
    factors[me] = jnp.broadcast_to(jnp.sqrt(column), (own, LANES))
    out_copies = []
    for i in range(1, devices):
        there, coords = device(i)
        copy = pltpu.make_async_remote_copy(
            place.at[there], place_recv.at[i], pl_send.at[i], pl_got.at[i],
            device_id=coords, device_id_type=MESH,
        )
        copy.start()
        out_copies.append(copy)
    for i in range(1, n_member):
        copy = pltpu.make_async_remote_copy(
            factors.at[me], factors.at[me], f_send.at[i], f_got.at[i],
            device_id=peer(i), device_id_type=MESH,
        )
        copy.start()
        ag.append(copy)
    for copy in ag:
        copy.wait_recv()

    @pl.loop(0, n_member)
    def _(k):
        @pl.loop(0, own, unroll=8)
        def _(r):
            start = pl.multiple_of((k * own + r) * LANES, LANES)
            wide = ens[:, pl.ds(start, LANES)].astype(F32)
            at = means[k, pl.ds(r, 1), :]
            out_ref[:, pl.ds(start, LANES)] = (
                at + factors[k, pl.ds(r, 1), :] * (wide - at)
            ).astype(BF16)

    for copy in out_copies:
        copy.wait_recv()
    result = place[flat]
    for i in range(1, devices):
        result = result + place_recv[i]
    post_ref[...] = result[:, :share]
    for copy in rs + rs_rest + ag + out_copies:
        copy.wait_send()


def body(n_region, n_member, ensemble, obs_value, obs_var, obs_point, owned, infl_mean, infl_var):
    members = ensemble.shape[0] * n_member
    slots = owned.shape[0]
    own = slots // n_member
    blocks = infl_mean.shape[0]
    devices = n_region * n_member
    share = blocks // devices
    owned = owned.reshape(1, slots)
    infl_mean = infl_mean.reshape(-1, LANES)
    infl_var = infl_var.reshape(-1, LANES)
    operands = (ensemble, obs_value, obs_var, obs_point, owned, infl_mean, infl_var)
    dma = pltpu.SemaphoreType.DMA
    operands = tuple(pltpu.with_memory_space_constraint(x, pltpu.HBM) for x in operands)
    inflated, post = pl.pallas_call(
        functools.partial(kernel, n_region, n_member, members),
        out_shape=(
            jax.ShapeDtypeStruct(ensemble.shape, BF16),
            jax.ShapeDtypeStruct((1, share), F32),
        ),
        in_specs=[pl.BlockSpec(memory_space=pltpu.HBM)] * len(operands),
        out_specs=(
            pl.BlockSpec(memory_space=pltpu.VMEM),
            pl.BlockSpec(memory_space=pltpu.VMEM),
        ),
        scratch_shapes=[pltpu.VMEM(a.shape, a.dtype) for a in operands]
        + [
            pltpu.VMEM((n_member, 5 * own + 8, LANES), F32),
            pltpu.VMEM((n_member, 5 * own + 8, LANES), F32),
            pltpu.VMEM((n_member, own, LANES), F32),
            pltpu.VMEM((n_member, own, LANES), F32),
            pltpu.VMEM((5 * (slots // 2), 2 * LANES), F32),
            pltpu.VMEM((8, slots), F32),
            pltpu.VMEM((devices, 1, LANES), F32),
            pltpu.VMEM((devices, 1, LANES), F32),
            dma((len(operands),)),
            dma((2, n_member)), dma((2, n_member)),
            dma((n_member,)), dma((n_member,)),
            dma((n_member,)), dma((n_member,)),
            dma((devices,)), dma((devices,)),
        ],
        compiler_params=pltpu.CompilerParams(collective_id=0, has_side_effects=True, vmem_limit_bytes=12*2**20),
    )(*operands)
    return inflated, post.reshape(share)


def solution(mesh):
    placed = (
        P("member", "region"),
        P(("region", "member"), None),
        P(("region", "member"), None),
        P(("region", "member"), None),
        P("region"),
        P(),
        P(),
    )
    return jax.shard_map(
        functools.partial(body, mesh.shape["region"], mesh.shape["member"]),
        mesh=mesh,
        in_specs=placed,
        out_specs=(P("member", "region"), P(("region", "member"))),
        check_vma=False,
    )
```

profile of v0, /device:TPU:1, one launch (start us, length us, event | category | flops | bytes accessed | tf_op | source)
XLA Modules:
  0.0 37.6 jit_solution(12767878743397182461)
XLA Ops:
  0.6 35.7 %shard_map.86 = (bf16[10,16384]{1,0:T(8,128)(2,1)S(1)}, f32[1,16]{1,0:T(1,128)S(1)}) custom-call(bf16[10,16384]{1,0:T(8,128)(2,1)} %ens_hbm.1, f32[32,128]{1,0:T(8,128)} %value_hbm.1, f32[32,128]{1,0:T(8,128)} %var_hbm.1, s32[32,128]{1,0:T(8,128)} %point_hbm.1, s32[1,128]{1,0:T(1,128)} %bitcast.7, f32[32,128]{1,0:T(8,128)} %bitcast.5, f32[32,128]{1,0:T(8,128)} %bitcast.6), custom_call_target="tpu_custom_call" | custom-call | tf_op jit(solution)/shard_map/pallas_call | solution.py:297
  36.3 0.8 %copy.11 = bf16[10,16384]{1,0:T(8,128)(2,1)} copy(bf16[10,16384]{1,0:T(8,128)(2,1)S(1)} %get-tuple-element.8) | data formatting | bytes 655360
  37.1 0.5 %copy.12 = f32[16]{0:T(128)} copy(f32[16]{0:T(128)S(1)} %bitcast.4) | data formatting | bytes 128
where the time goes:
time: 37.7 us; the launch traced here: 37.6 us
  Pallas kernels  35.7 us (95%)
  local copies, waits for them, and re-layouts  1.31 us (3%)
  between operations  0.64 us (2%)
    pallas_call x1, Pallas kernels, body(): pl.pallas_call(functools.partial(kernel, n_region, n_member, members), ou...  35.7 us
    unnamed x2, local copies, waits for them, and re-layouts  1.31 us

commit v1 on v0

--- a/solution.py
+++ b/solution.py
@@ -23,7 +23,7 @@
     return terms
 
 
-def scatter(value_ref, var_ref, point_ref, acc, row_acc, half, first_part):
+def scatter(value_ref, var_ref, point_ref, acc, row_acc, half):
     rows = point_ref.shape[0]
     step = 8
     low_ids = lax.broadcasted_iota(jnp.int32, (half, LANES), 0)
@@ -69,13 +69,10 @@
         acc[...] += points
         row_acc[...] += by_slot
 
-    if first_part:
-        points, by_slot = chunk(0)
-        acc[...] = points
-        row_acc[...] = by_slot
-        pl.loop(1, rows // step // 2)(add)
-    else:
-        pl.loop(rows // step // 2, rows // step)(add)
+    points, by_slot = chunk(0)
+    acc[...] = points
+    row_acc[...] = by_slot
+    pl.loop(1, rows // step)(add)
 
 
 def kernel(
@@ -84,7 +81,7 @@
     out_ref, post_ref,
     ens, value, var, point, owned, pmean, pvar,
     part, rs_recv, means, factors, acc, row_acc, place, place_recv,
-    in_sem, rs_send, rs_got, mean_send, mean_got, f_send, f_got, pl_send, pl_got,
+    in_sem, send_sem, got_sem,
 ):
     region = lax.axis_index("region")
     me = lax.axis_index("member")
@@ -94,16 +91,6 @@
     devices = n_region * n_member
     flat = region * n_member + me
 
-    def device(i):
-        there = lax.rem(flat + i, devices)
-        return there, (there // n_member, lax.rem(there, n_member))
-
-    def peer(i):
-        return {"member": lax.rem(me + i, n_member)}
-
-    barrier = pltpu.get_barrier_semaphore()
-    for i in range(1, devices):
-        pl.semaphore_signal(barrier, inc=1, device_id=device(i)[1], device_id_type=MESH)
     pairs = (
         (ens_hbm, ens), (point_hbm, point), (value_hbm, value), (var_hbm, var),
         (owned_hbm, owned), (pmean_hbm, pmean), (pvar_hbm, pvar),
@@ -111,6 +98,14 @@
     loads = [pltpu.make_async_copy(s, d, in_sem.at[i]) for i, (s, d) in enumerate(pairs)]
     for load in loads:
         load.start()
+
+    member_at = [me] + [lax.rem(me + j, n_member) for j in range(1, n_member)]
+    region_at = [region] + [lax.rem(region + k, n_region) for k in range(1, n_region)]
+    barrier = pltpu.get_barrier_semaphore()
+    for j in range(1, n_member):
+        pl.semaphore_signal(barrier, inc=1, device_id=(region, member_at[j]), device_id_type=MESH)
+    for k in range(1, n_region):
+        pl.semaphore_signal(barrier, inc=1, device_id=(region_at[k], me), device_id_type=MESH)
     loads[0].wait()
 
     @pl.loop(0, n_member)
@@ -122,26 +117,28 @@
             part[k, pl.ds(r, 1), :] = jnp.sum(wide, 0, keepdims=True)
             part[k, pl.ds(own + r, 1), :] = jnp.sum(wide * wide, 0, keepdims=True)
 
+    pl.semaphore_wait(barrier, n_member - 1 + n_region - 1)
+
+    def send(src, dst, phase, coords):
+        pltpu.make_async_remote_copy(
+            src, dst, send_sem.at[phase], got_sem.at[phase], device_id=coords, device_id_type=MESH
+        ).start()
+
+    def drain(ref, sem):
+        pltpu.make_async_copy(ref, ref, sem).wait()
+
+    def reduce_copies(first, count, phase):
+        for i in range(1, n_member):
+            there = member_at[i]
+            send(
+                part.at[there, pl.ds(first, count), :], rs_recv.at[i, pl.ds(first, count), :],
+                phase, (region, there),
+            )
+
+    reduce_copies(0, 2 * own, 0)
     for load in loads[1:]:
         load.wait()
-    scatter(value, var, point, acc, row_acc, half, True)
-    pl.semaphore_wait(barrier, devices - 1)
-
-    def reduce_copies(first, count, which):
-        copies = []
-        for i in range(1, n_member):
-            copy = pltpu.make_async_remote_copy(
-                part.at[lax.rem(me + i, n_member), pl.ds(first, count), :],
-                rs_recv.at[i, pl.ds(first, count), :],
-                rs_send.at[which, i], rs_got.at[which, i],
-                device_id=peer(i), device_id_type=MESH,
-            )
-            copy.start()
-            copies.append(copy)
-        return copies
-
-    rs = reduce_copies(0, 2 * own, 0)
-    scatter(value, var, point, acc, row_acc, half, False)
+    scatter(value, var, point, acc, row_acc, half)
 
     for index, (first, last) in enumerate(((0, 1), (1, 3), (3, 5))):
         both = acc[first * half : (first + 1) * half, :]
@@ -163,7 +160,7 @@
     for k in range(n_member):
         part[k, 5 * own :, :] = rows
 
-    rs_rest = reduce_copies(2 * own, 3 * own + 8, 1)
+    reduce_copies(2 * own, 3 * own + 8, 1)
 
     block = owned[...]
     groups = pmean.shape[0]
@@ -193,29 +190,22 @@
         lax.broadcasted_iota(jnp.int32, (own, slots), 0) + own * me
     )
 
-    for copy in rs:
-        copy.wait_recv()
+    others = pl.ds(1, n_member - 1)
+    drain(rs_recv.at[others, pl.ds(0, 2 * own), :], got_sem.at[0])
 
     def reduced(first, last):
-        total = part[me, first:last, :]
-        for i in range(1, n_member):
-            total = total + rs_recv[i, first:last, :]
-        return total
+        terms = [part[me, first:last, :]] + [rs_recv[i, first:last, :] for i in range(1, n_member)]
+        while len(terms) > 1:
+            terms = [a + b for a, b in zip(terms[::2], terms[1::2])]
+        return terms[0]
 
     both = reduced(0, 2 * own)
     mean = both[:own] / members
     means[me] = mean
-    ag = []
     for i in range(1, n_member):
-        copy = pltpu.make_async_remote_copy(
-            means.at[me], means.at[me], mean_send.at[i], mean_got.at[i],
-            device_id=peer(i), device_id_type=MESH,
-        )
-        copy.start()
-        ag.append(copy)
+        send(means.at[me], means.at[me], 2, (region, member_at[i]))
     spread = (both[own:] - members * mean * mean) / (members - 1)
-    for copy in rs_rest:
-        copy.wait_recv()
+    drain(rs_recv.at[others, pl.ds(2 * own, 3 * own + 8), :], got_sem.at[1])
     count = reduced(2 * own, 3 * own)
     y_sum = reduced(3 * own, 4 * own)
     v_sum = reduced(4 * own, 5 * own)
@@ -241,24 +231,17 @@
         place[d] = placed[d : d + 1]
     column = jnp.sum(jnp.where(mine, post, 0.0), axis=1, keepdims=True)
     factors[me] = jnp.broadcast_to(jnp.sqrt(column), (own, LANES))
-    out_copies = []
-    for i in range(1, devices):
-        there, coords = device(i)
-        copy = pltpu.make_async_remote_copy(
-            place.at[there], place_recv.at[i], pl_send.at[i], pl_got.at[i],
-            device_id=coords, device_id_type=MESH,
-        )
-        copy.start()
-        out_copies.append(copy)
+    for k in sorted(range(n_region), key=lambda k: -min(k % 8, 8 - k % 8) - min(k // 8, 4 - k // 8)):
+        for j in range(n_member):
+            if k or j:
+                send(
+                    place.at[region_at[k] * n_member + member_at[j]], place_recv.at[k * n_member + j],
+                    3, (region_at[k], member_at[j]),
+                )
     for i in range(1, n_member):
-        copy = pltpu.make_async_remote_copy(
-            factors.at[me], factors.at[me], f_send.at[i], f_got.at[i],
-            device_id=peer(i), device_id_type=MESH,
-        )
-        copy.start()
-        ag.append(copy)
-    for copy in ag:
-        copy.wait_recv()
+        send(factors.at[me], factors.at[me], 4, (region, member_at[i]))
+    drain(means.at[others], got_sem.at[2])
+    drain(factors.at[others], got_sem.at[4])
 
     @pl.loop(0, n_member)
     def _(k):
@@ -271,14 +254,17 @@
                 at + factors[k, pl.ds(r, 1), :] * (wide - at)
             ).astype(BF16)
 
-    for copy in out_copies:
-        copy.wait_recv()
-    result = place[flat]
-    for i in range(1, devices):
-        result = result + place_recv[i]
-    post_ref[...] = result[:, :share]
-    for copy in rs + rs_rest + ag + out_copies:
-        copy.wait_send()
+    drain(rs_recv.at[others, pl.ds(0, 2 * own), :], send_sem.at[0])
+    drain(rs_recv.at[others, pl.ds(2 * own, 3 * own + 8), :], send_sem.at[1])
+    drain(means.at[others], send_sem.at[2])
+    drain(factors.at[others], send_sem.at[4])
+    rest = pl.ds(1, devices - 1)
+    drain(place_recv.at[rest], got_sem.at[3])
+    terms = [place[flat]] + [place_recv[i] for i in range(1, devices)]
+    while len(terms) > 1:
+        terms = [a + b for a, b in zip(terms[::2], terms[1::2])]
+    post_ref[...] = terms[0][:, :share]
+    drain(place_recv.at[rest], send_sem.at[3])
 
 
 def body(n_region, n_member, ensemble, obs_value, obs_var, obs_point, owned, infl_mean, infl_var):
@@ -316,10 +302,7 @@
             pltpu.VMEM((devices, 1, LANES), F32),
             pltpu.VMEM((devices, 1, LANES), F32),
             dma((len(operands),)),
-            dma((2, n_member)), dma((2, n_member)),
-            dma((n_member,)), dma((n_member,)),
-            dma((n_member,)), dma((n_member,)),
-            dma((devices,)), dma((devices,)),
+            dma((5,)), dma((5,)),
         ],
         compiler_params=pltpu.CompilerParams(collective_id=0, has_side_effects=True, vmem_limit_bytes=12*2**20),
     )(*operands)

time: 37.7 us -> 28.2 us (0.75)
  Pallas kernels: 35.7 us -> 26.1 us
    pallas_call x1, Pallas kernels: 35.7 us -> 26.1 us  [body(): pl.pallas_call(functools.partial(kernel, n_region, n_member, members), ou...]
where the time goes in v1:
time: 28.2 us; the launch traced here: 28.1 us
  Pallas kernels  26.1 us (93%)
  local copies, waits for them, and re-layouts  1.31 us (5%)
  between operations  0.64 us (2%)
    pallas_call x1, Pallas kernels, body(): pl.pallas_call(functools.partial(kernel, n_region, n_member, members), ou...  26.1 us
    unnamed x2, local copies, waits for them, and re-layouts  1.31 us

profile of v1, /device:TPU:1, one launch (start us, length us, event | category | flops | bytes accessed | tf_op | source)
XLA Modules:
  0.0 28.1 jit_solution(16337934546884248066)
XLA Ops:
  0.6 26.1 %shard_map.86 = (bf16[10,16384]{1,0:T(8,128)(2,1)S(1)}, f32[1,16]{1,0:T(1,128)S(1)}) custom-call(bf16[10,16384]{1,0:T(8,128)(2,1)} %ens_hbm.1, f32[32,128]{1,0:T(8,128)} %value_hbm.1, f32[32,128]{1,0:T(8,128)} %var_hbm.1, s32[32,128]{1,0:T(8,128)} %point_hbm.1, s32[1,128]{1,0:T(1,128)} %bitcast.7, f32[32,128]{1,0:T(8,128)} %bitcast.5, f32[32,128]{1,0:T(8,128)} %bitcast.6), custom_call_target="tpu_custom_call" | custom-call | tf_op jit(solution)/shard_map/pallas_call | solution.py:283
  26.8 0.8 %copy.11 = bf16[10,16384]{1,0:T(8,128)(2,1)} copy(bf16[10,16384]{1,0:T(8,128)(2,1)S(1)} %get-tuple-element.8) | data formatting | bytes 655360
  27.6 0.5 %copy.12 = f32[16]{0:T(128)} copy(f32[16]{0:T(128)S(1)} %bitcast.4) | data formatting | bytes 128
